TPU v7x, 32 devices: a whole 2x2x4 slice. The times are simulated.
32 devices in a mesh: struct: 8 (over z, x), atom: 4 (over y, core).
Axes of the slice: x: 2, y: 2, z: 4, core: 2. Of those that a mesh axis runs over, the one named last changes fastest.
Arguments:
- atoms_in: bfloat16 [32, 1536, 128], P('struct', 'atom'), parts along dimension 0, may hold values from -6 to 6
- cond: bfloat16 [12288, 128], P(('struct', 'atom')), parts along dimension 0, may hold values from -6 to 6
- pair: bfloat16 [384, 32, 16, 128], P(('struct', 'atom')), parts along dimension 0, may hold values from -6 to 6
- atom_mask: int32 [12288], P(('struct', 'atom')), parts along dimension 0, may hold values 0 or 1
- atom_count: int32 [8], P('struct'), parts along dimension 0, may hold values from 1344 to 1536
- atom_to_token: int32 [12288], P(('struct', 'atom')), parts along dimension 0, may hold values from 0 to 191, as said below
- ada_weight: bfloat16 [2, 128, 256], replicated, may hold values from -0.5 to 0.5
- ada_bias: float32 [2, 128], replicated, may hold values from -1.5 to 1.5
- zero_weight: bfloat16 [2, 128, 128], replicated, may hold values from -0.5 to 0.5
- zero_bias: float32 [2, 128], replicated, may hold values from -2 to 2
- qkvg_weight: bfloat16 [128, 512], replicated, may hold values from -0.5 to 0.5
- query_bias: float32 [128], replicated, may hold values from -4 to 4
- pair_weight: float32 [4, 16], replicated, may hold values from -60 to 60
- out_weight: bfloat16 [128, 128], replicated, may hold values from -0.5 to 0.5
- swiglu_weight: bfloat16 [128, 512], replicated, may hold values from -0.5 to 0.5
- down_weight: bfloat16 [256, 128], replicated, may hold values from -0.375 to 0.375
- token_weight: bfloat16 [128, 768], replicated, may hold values from -0.5 to 0.5
Outputs:
- atoms_out: bfloat16 [32, 1536, 128], P('struct', 'atom'), parts along dimension 0
- tokens_out: bfloat16 [32, 192, 768], P('struct', 'atom'), parts along dimension 0
There are 8 independent parts, one for each index of `struct`. A program takes and returns all parts, laid end to end along the dimension named above; an argument that names none is the same for every part. Nothing has to cross between parts.
Inputs may be any that keep to these rules, and one draw needn't show every extreme that they name: `atom_to_token`: never falls, rises by at most 1 from atom to atom, starts at 0 and ends at 191; an atom a of token t satisfies 8 * t - 8 < a < 8 * t + 2 * 8 - 1.
All inputs are finite; a program needn't handle non-finite values. No bound on the sum of `atom_mask` on one device may be relied on, other than what follows from the above.
Results may differ from a plain program's by a relative error of at most 0.01.
Values may be sent and summed in bfloat16 or wider, within the bound.
A program may use at most 64 MiB of HBM per device.

v0:
```python
import jax
import jax.numpy as jnp
from jax import lax
from jax.sharding import PartitionSpec as P

ATOMS_PER_TOKEN = 8


EPS = 1e-05


def extended_2(shard, sides, width):
    for axis, dim in sides:
        count, length = (lax.axis_size(axis), shard.shape[dim])
        up = [(i, (i + 1) % count) for i in range(count - 1)]
        down = [(j, i) for i, j in up]
        last = lax.slice_in_dim(shard, length - width, length, axis=dim)
        initial = lax.slice_in_dim(shard, 0, width, axis=dim)
        before = lax.ppermute(last, axis, up)
        after = lax.ppermute(initial, axis, down)
        shard = jnp.concatenate([before, shard, after], axis=dim)
    return shard


def layer_norm(values, along=-1):
    center = jnp.mean(values, along, keepdims=True)
    spread = jnp.mean(jnp.square(values - center), along, keepdims=True)
    return (values - center) * lax.rsqrt(spread + EPS)


def window_view(extended, windows_here, query_len, reach):
    blocks = extended.reshape(
        (extended.shape[0], windows_here + reach - 1, query_len) + extended.shape[2:]
    )
    return jnp.concatenate(
        [blocks[:, offset : offset + windows_here] for offset in range(reach)], axis=2
    )


def on_device(
    atoms_in,
    cond,
    pair,
    atom_mask,
    atom_count,
    atom_to_token,
    ada_weight,
    ada_bias,
    zero_weight,
    zero_bias,
    qkvg_weight,
    query_bias,
    pair_weight,
    out_weight,
    swiglu_weight,
    down_weight,
    token_weight,
):
    samples, atom_dev, model_width = atoms_in.shape
    head_count = pair_weight.shape[0]
    head_dim = model_width // head_count
    query_len = pair.shape[1]
    key_len = pair.shape[3]
    reach = key_len // query_len
    margin = (key_len - query_len) // 2
    windows_here = atom_dev // query_len
    tok_dev = atom_dev // ATOMS_PER_TOKEN
    device_pos = lax.axis_index("atom")
    start_atom = device_pos * atom_dev
    atoms_total = lax.axis_size("atom") * atom_dev
    integers = jnp.stack([atom_mask, atom_to_token])
    integers_ext = extended_2(integers, (("atom", 1),), margin)
    ext_positions = start_atom - margin + jnp.arange(atom_dev + 2 * margin, dtype=jnp.int32)
    usable_ext = (
        (integers_ext[0] == 1)
        & (ext_positions >= 0)
        & (ext_positions < atoms_total)
        & (ext_positions < atom_count[0])
    )
    usable_local = usable_ext[margin : margin + atom_dev]
    cond_norm = layer_norm(cond.astype(jnp.float32)).astype(jnp.bfloat16)
    adapt = [
        jnp.dot(cond_norm, ada_weight[which], preferred_element_type=jnp.float32)
        for which in range(2)
    ]
    gating = [
        jax.nn.sigmoid(
            jnp.dot(cond_norm, zero_weight[which], preferred_element_type=jnp.float32)
            + zero_bias[which]
        )
        for which in range(2)
    ]

    def adaptive(stream, which):
        return (
            layer_norm(stream) * jax.nn.sigmoid(adapt[which][:, :model_width] + ada_bias[which])
            + adapt[which][:, model_width:]
        )

    attn_in = adaptive(atoms_in.astype(jnp.float32), 0).astype(jnp.bfloat16)
    projected = jnp.dot(attn_in, qkvg_weight, preferred_element_type=jnp.float32)
    factor = head_dim ** (-0.5)
    queries = ((projected[..., :model_width] + query_bias) * factor).astype(jnp.bfloat16)
    gate_attn = jax.nn.sigmoid(projected[..., 3 * model_width :])
    keyval_local = projected[..., model_width : 3 * model_width].astype(jnp.bfloat16)
    keyval = extended_2(keyval_local, (("atom", 1),), margin)
    windowed = window_view(keyval, windows_here, query_len, reach)
    key_live = window_view(usable_ext[None], windows_here, query_len, reach)[0]
    pair_norm = layer_norm(pair.astype(jnp.float32), 2)
    pair_bias = jnp.einsum("wicj,hc->whij", pair_norm, pair_weight, precision=lax.Precision.HIGHEST)
    query_win = queries.reshape(samples, windows_here, query_len, head_count, head_dim)
    keys_win = windowed[..., :model_width].reshape(
        samples, windows_here, key_len, head_count, head_dim
    )
    values_win = windowed[..., model_width:].reshape(
        samples, windows_here, key_len, head_count, head_dim
    )
    scores = (
        jnp.einsum("bwihd,bwjhd->bwhij", query_win, keys_win, preferred_element_type=jnp.float32)
        + pair_bias[None]
    )
    scores = jnp.where(key_live[None, :, None, None, :], scores, -1000000000.0)
    attention = jax.nn.softmax(scores, axis=-1).astype(jnp.bfloat16)
    weighted = jnp.einsum(
        "bwhij,bwjhd->bwihd", attention, values_win, preferred_element_type=jnp.float32
    )
    blended = (weighted.reshape(samples, atom_dev, model_width) * gate_attn).astype(jnp.bfloat16)
    after_attn = (
        atoms_in.astype(jnp.float32)
        + gating[0] * jnp.dot(blended, out_weight, preferred_element_type=jnp.float32)
    ).astype(jnp.bfloat16)
    trans_in = adaptive(after_attn.astype(jnp.float32), 1).astype(jnp.bfloat16)
    mixed = jnp.dot(trans_in, swiglu_weight, preferred_element_type=jnp.float32)
    hidden_units = mixed.shape[-1] // 2
    hidden = (jax.nn.silu(mixed[..., :hidden_units]) * mixed[..., hidden_units:]).astype(
        jnp.bfloat16
    )
    atoms_out = (
        after_attn.astype(jnp.float32)
        + gating[1] * jnp.dot(hidden, down_weight, preferred_element_type=jnp.float32)
    ).astype(jnp.bfloat16)
    features = jax.nn.relu(
        jnp.dot(atoms_out, token_weight, preferred_element_type=jnp.float32)
    ).astype(jnp.bfloat16)
    token_base = device_pos * tok_dev - 1
    slots = jnp.arange(tok_dev + 2, dtype=jnp.int32)
    relative_local = atom_to_token - token_base
    onehot_local = ((relative_local[:, None] == slots[None, :]) & usable_local[:, None]).astype(
        jnp.bfloat16
    )
    totals = jnp.einsum("at,bac->btc", onehot_local, features, preferred_element_type=jnp.float32)
    relative_ext = integers_ext[1] - token_base
    counts = jnp.sum(
        ((relative_ext[:, None] == slots[None, :]) & usable_ext[:, None]).astype(jnp.float32),
        axis=0,
    )
    lower_row = totals[:, 0]
    upper_row = totals[:, tok_dev + 1]
    edges_sums = extended_2(jnp.stack([lower_row, upper_row], axis=1), (("atom", 1),), 1)
    from_left = edges_sums[:, 0]
    from_right = edges_sums[:, 3]
    local_rows = totals[:, 1 : tok_dev + 1]
    first_row = local_rows[:, :1] + from_left[:, None]
    last_row = local_rows[:, tok_dev - 1 :] + from_right[:, None]
    local_rows = jnp.concatenate([first_row, local_rows[:, 1 : tok_dev - 1], last_row], axis=1)
    tokens_out = (local_rows / jnp.maximum(counts[1 : tok_dev + 1], 1.0)[None, :, None]).astype(
        jnp.bfloat16
    )
    return (atoms_out, tokens_out)


def solution(mesh):
    in_specs = (
        P("struct", "atom", None),
        P(("struct", "atom"), None),
        P(("struct", "atom"), None, None, None),
        P(("struct", "atom")),
        P("struct"),
        P(("struct", "atom")),
        P(),
        P(),
        P(),
        P(),
        P(),
        P(),
        P(),
        P(),
        P(),
        P(),
        P(),
    )
    out_specs = (P("struct", "atom", None), P("struct", "atom", None))
    return jax.shard_map(
        on_device, mesh=mesh, in_specs=in_specs, out_specs=out_specs, check_vma=False
    )
```

profile of v0, /device:TPU:1, one launch (start us, length us, event | category | flops | bytes accessed | tf_op | source)
XLA Modules:
  0.0 67.2 jit_solution(8746185659331445704)
XLA Ops:
  0.6 0.0 copy-start
  0.7 1.1 %convert_reduce_fusion.2 = f32[384]{0:T(512)S(1)} fusion(bf16[384,128]{1,0:T(8,128)(2,1)} %param.18), kind=kLoop, calls=%fused_computation.80 | loop fusion | flops 97920 | bytes 99840 | tf_op jit(solution)/shard_map/reduce_sum | solution.py:26
  1.7 1.1 %fusion.67 = f32[384]{0:T(512)S(1)} fusion(bf16[384,128]{1,0:T(8,128)(2,1)} %param.18, f32[384]{0:T(512)S(1)} %broadcast_multiply_fusion.3), kind=kLoop, calls=%fused_computation.83 | loop fusion | flops 196224 | bytes 101376 | tf_op jit(solution)/shard_map/reduce_sum | solution.py:27
  2.9 1.2 %fusion.86 = f32[384,256]{1,0:T(8,128)S(1)} fusion(bf16[2,128,256]{2,1,0:T(8,128)(2,1)} %param.23, bf16[384,128]{1,0:T(8,128)(2,1)} %param.18, f32[384]{0:T(512)S(1)} %add_rsqrt_fusion.3, f32[384]{0:T(512)S(1)} %broadcast_multiply_fusion.3), kind=kOutput, calls=%fused_computation.107 | convolution fusion | flops 25362432 | bytes 560128 | tf_op jit(solution)/shard_map/dot_general | solution.py:83
  4.1 1.2 %fusion.88 = f32[384,256]{1,0:T(8,128)S(1)} fusion(bf16[2,128,256]{2,1,0:T(8,128)(2,1)} %param.23, bf16[384,128]{1,0:T(8,128)(2,1)} %param.18, f32[384]{0:T(512)S(1)} %add_rsqrt_fusion.3, f32[384]{0:T(512)S(1)} %broadcast_multiply_fusion.3), kind=kOutput, calls=%fused_computation.109 | convolution fusion | flops 25362432 | bytes 560128 | tf_op jit(solution)/shard_map/dot_general | solution.py:83
  5.2 1.2 %copy.36 = bf16[4,384,128]{1,2,0:T(8,128)(2,1)S(1)} copy(bf16[4,384,128]{2,1,0:T(8,128)(2,1)} %param.17) | data formatting | bytes 786432 | tf_op args[0]
  6.5 0.8 %slice_bitcast_fusion = (f32[128]{0:T(128)S(1)}, f32[128]{0:T(128)S(1)}) fusion(f32[2,128]{1,0:T(2,128)} %param.24), kind=kLoop, calls=%fused_computation.151 | loop fusion | bytes 2048 | tf_op jit(solution)/shard_map/add | solution.py:96
  7.2 0.1 fusion.72
  7.4 0.1 copy.39
  7.5 0.1 copy.38
  7.6 0.1 convert_reduce_fusion.1
  7.7 0.0 copy-start.13
  7.7 0.1 fusion.39
  7.9 0.0 copy-start.15
  7.9 0.6 fusion.124
  8.5 0.7 %fusion.121 = (bf16[4,48,256]{2,1,0:T(8,128)(2,1)}, bf16[4,48,256]{2,1,0:T(8,128)(2,1)}) fusion(bf16[4,384,512]{2,1,0:T(8,128)(2,1)S(1)} %get-tuple-element.30), kind=kLoop, calls=%fused_computation.160 | loop fusion | bytes 393216 | tf_op jit(solution)/shard_map/slice | solution.py:17
  9.2 2.2 %collective-permute-start.1 = (bf16[4,48,256]{2,1,0:T(8,128)(2,1)}, bf16[4,48,256]{2,1,0:T(8,128)(2,1)}, u32[]{:S(2)}, u32[]{:S(2)}) collective-permute-start(bf16[4,48,256]{2,1,0:T(8,128)(2,1)} %get-tuple-element.9), channel_id=1, source_target_pairs={{1,0},{2,1},{3,2},{5,4},{6,5},{7,6},{9,8},{10,9},{11,10},{13,12},{... | collective-permute-start | bytes 294920 | tf_op jit(solution)/shard_map/ppermute | solution.py:20
  11.4 4.5 %collective-permute-start = (bf16[4,48,256]{2,1,0:T(8,128)(2,1)}, bf16[4,48,256]{2,1,0:T(8,128)(2,1)}, u32[]{:S(2)}, u32[]{:S(2)}) collective-permute-start(bf16[4,48,256]{2,1,0:T(8,128)(2,1)} %get-tuple-element.8), channel_id=1, source_target_pairs={{0,1},{1,2},{2,3},{4,5},{5,6},{6,7},{8,9},{9,10},{10,11},{12,13},{... | collective-permute-start | bytes 294920 | tf_op jit(solution)/shard_map/ppermute | solution.py:19
  16.0 0.7 pad_add_fusion.2
  16.7 1.9 %collective-permute-start.3 = (s32[2,48]{1,0:T(2,128)}, s32[2,48]{1,0:T(2,128)S(1)}, u32[]{:S(2)}, u32[]{:S(2)}) collective-permute-start(s32[2,48]{1,0:T(2,128)} %get-tuple-element.21), channel_id=1, source_target_pairs={{1,0},{2,1},{3,2},{5,4},{6,5},{7,6},{9,8},{10,9},{11,10},{13,12},{... | collective-permute-start | bytes 1160 | tf_op jit(solution)/shard_map/ppermute | solution.py:20
  18.6 3.6 %collective-permute-start.2 = (s32[2,48]{1,0:T(2,128)}, s32[2,48]{1,0:T(2,128)}, u32[]{:S(2)}, u32[]{:S(2)}) collective-permute-start(s32[2,48]{1,0:T(2,128)} %get-tuple-element.20), channel_id=1, source_target_pairs={{0,1},{1,2},{2,3},{4,5},{5,6},{6,7},{8,9},{9,10},{10,11},{12,13},{... | collective-permute-start | bytes 1160 | tf_op jit(solution)/shard_map/ppermute | solution.py:19
  22.2 0.1 slice.170
  22.3 0.1 fusion.48
  22.4 1.8 %reshape.153 = bf16[4,12,32,4,32]{4,3,2,1,0:T(4,128)(2,1)} reshape(bf16[4,384,128]{2,1,0:T(8,128)(2,1)S(1)} %fusion.48) | data formatting | bytes 786432 | tf_op jit(solution)/shard_map/reshape | solution.py:111
  24.2 0.7 %convert_reduce_fusion = f32[12,32,128]{2,1,0:T(8,128)S(1)} fusion(bf16[12,32,16,128]{3,2,1,0:T(8,128)(2,1)S(1)} %copy-done.1), kind=kLoop, calls=%fused_computation.3 | loop fusion | flops 1523712 | bytes 1769472 | tf_op jit(solution)/shard_map/reduce_sum | solution.py:26
  25.0 1.0 %fusion.3 = f32[12,32,128]{2,1,0:T(8,128)S(1)} fusion(bf16[12,32,16,128]{3,2,1,0:T(8,128)(2,1)S(1)} %copy-done.1, f32[12,32,128]{2,1,0:T(8,128)S(1)} %broadcast_multiply_fusion), kind=kLoop, calls=%fused_computation.6 | loop fusion | flops 3096576 | bytes 1966080 | tf_op jit(solution)/shard_map/reduce_sum | solution.py:27
  26.0 2.0 %fusion.20 = f32[12,4,32,128]{3,1,2,0:T(4,128)S(1)} fusion(bf16[12,32,16,128]{3,2,1,0:T(8,128)(2,1)S(1)} %copy-done.1, f32[12,32,128]{2,1,0:T(8,128)S(1)} %add_rsqrt_fusion, f32[12,32,128]{2,1,0:T(8,128)S(1)} %broadcast_multiply_fusion, f32[4,16]{1,0:T(4,128)S(1)} %copy-done.12), kind=kOutput, calls=%fused_computation.27 | convolution fusion | flops 40108032 | bytes 2752768 | tf_op jit(solution)/shard_map/wicj,hc->whij/dot_general | solution.py:110
  28.1 1.0 %copy.44 = f32[12,4,32,128]{3,2,1,0:T(8,128)} copy(f32[12,4,32,128]{3,1,2,0:T(4,128)S(1)} %fusion.20) | data formatting | bytes 1572864 | tf_op jit(solution)/shard_map/wicj,hc->whij/transpose | solution.py:110
  29.8 0.3 fusion.32
  30.1 0.8 %copy.37 = f32[384,128]{0,1:T(8,128)} copy(f32[384,128]{1,0:T(8,128)S(1)} %fusion.32) | data formatting | bytes 393216 | tf_op jit(solution)/shard_map/div | solution.py:87
  30.9 0.3 fusion.36
  31.2 0.1 copy.49
  31.3 0.8 %copy.48 = f32[384,128]{0,1:T(8,128)} copy(f32[384,128]{1,0:T(8,128)S(1)} %get-tuple-element.16) | data formatting | bytes 393216 | tf_op jit(solution)/shard_map/div | solution.py:87
  32.2 0.8 %copy.47 = f32[384,128]{0,1:T(8,128)} copy(f32[384,128]{1,0:T(8,128)S(1)} %fusion.36) | data formatting | bytes 393216 | tf_op jit(solution)/shard_map/div | solution.py:87
  33.0 0.7 %pad_add_fusion = s32[2,480]{1,0:T(2,128)S(1)} fusion(s32[2,48]{1,0:T(2,128)S(1)} %collective-permute-done.3, s32[1,384]{1,0:T(1,128)S(1)} %stack.10, s32[1,384]{1,0:T(1,128)S(1)} %stack.9, s32[2,48]{1,0:T(2,128)} %collective-permute-done.2), kind=kLoop, calls=%fused_computation.133 | loop fusion | flops 2880 | bytes 7680 | tf_op jit(solution)/shard_map/concatenate | solution.py:21
  33.7 0.1 eq.51
  33.9 0.7 slice.159
  34.5 0.1 add_bitcast_fusion
  34.6 1.0 %pad_maximum_fusion.1 = bf16[4,480,256]{2,1,0:T(8,128)(2,1)S(1)} fusion(bf16[4,48,256]{2,1,0:T(8,128)(2,1)} %collective-permute-done.1, bf16[4,384,256]{2,1,0:T(8,128)(2,1)S(1)} %slice.170, bf16[4,48,256]{2,1,0:T(8,128)(2,1)} %collective-permute-done), kind=kLoop, calls=%fused_computation.48 | loop fusion | flops 2949120 | bytes 1966080 | tf_op jit(solution)/shard_map/concatenate | solution.py:21
  35.6 0.4 fusion.122
  36.0 0.5 pad_maximum_fusion
  36.5 0.9 %fusion.120 = (bf16[4,12,128,128]{3,2,1,0:T(8,128)(2,1)S(1)}, bf16[4,12,128,128]{3,2,1,0:T(8,128)(2,1)S(1)}) fusion(bf16[4,12,128,256]{3,2,1,0:T(8,128)(2,1)S(1)} %pad_maximum_fusion), kind=kLoop, calls=%fused_computation.159 | loop fusion | bytes 6291456 | tf_op jit(solution)/shard_map/slice | solution.py:112
  37.5 1.6 %copy.41 = bf16[4,12,128,128]{2,3,1,0:T(8,128)(2,1)} copy(bf16[4,12,128,128]{3,2,1,0:T(8,128)(2,1)S(1)} %get-tuple-element.7) | data formatting | bytes 3145728 | tf_op jit(solution)/shard_map/slice | solution.py:115
  39.1 0.9 %copy.42 = bf16[4,12,128,128]{2,3,1,0:T(8,128)(2,1)S(1)} copy(bf16[4,12,128,128]{3,2,1,0:T(8,128)(2,1)S(1)} %get-tuple-element.6) | data formatting | bytes 3145728 | tf_op jit(solution)/shard_map/slice | solution.py:112
  40.0 2.0 %fusion.12 = f32[4,12,4,32,128]{4,3,2,1,0:T(8,128)S(1)} fusion(bf16[4,12,128,4,32]{2,4,3,1,0:T(8,128)(2,1)S(1)} %bitcast.67, bf16[4,12,32,4,32]{4,3,2,1,0:T(4,128)(2,1)} %reshape.153), kind=kOutput, calls=%fused_computation.19 | convolution fusion | flops 50331648 | bytes 5111808 | tf_op jit(solution)/shard_map/bwihd,bwjhd->bwhij/dot_general | solution.py:119
  42.1 3.0 %fusion.125 = (f32[4,12,4,32]{3,2,1,0:T(4,128)S(1)}, f32[4,12,4,32,128]{4,3,2,1,0:T(8,128)S(1)}) fusion(f32[4,12,4,32,128]{4,3,2,1,0:T(8,128)S(1)} %fusion.12, f32[12,4,32,128]{3,2,1,0:T(8,128)S(1)} %copy-done.4, pred[12,128]{1,0:T(8,128)(4,1)S(1)} %add_bitcast_fusion), kind=kOutput, calls=%fused_computation.164 | output fusion | flops 4718719 | bytes 7104000 | tf_op jit(solution)/shard_map/sub | solution.py:123
  45.1 2.4 %convolution_bitcast_fusion = f32[4,12,32,4,32]{2,4,3,1,0:T(8,128)} fusion(bf16[4,12,128,4,32]{2,4,3,1,0:T(8,128)(2,1)S(1)} %bitcast.68, f32[4,12,4,32,128]{4,3,2,1,0:T(8,128)S(1)} %get-tuple-element.33, f32[4,12,4,32]{3,2,1,0:T(4,128)S(1)} %get-tuple-element.32), kind=kOutput, calls=%fused_computation.16 | convolution fusion | flops 51904512 | bytes 5529600 | tf_op jit(solution)/shard_map/bwhij,bwjhd->bwihd/dot_general | solution.py:124
  47.5 3.3 %copy.45 = f32[4,12,32,4,32]{4,3,2,1,0:T(4,128)S(1)} copy(f32[4,12,32,4,32]{2,4,3,1,0:T(8,128)} %convolution_bitcast_fusion) | data formatting | bytes 1572864 | tf_op jit(solution)/shard_map/bwhij,bwjhd->bwihd/transpose | solution.py:124
  50.8 2.2 %reshape.155 = f32[4,384,128]{2,1,0:T(8,128)} reshape(f32[4,12,32,4,32]{4,3,2,1,0:T(4,128)S(1)} %copy.45) | data formatting | bytes 1572864 | tf_op jit(solution)/shard_map/reshape | solution.py:127
  53.0 2.0 %fusion.126 = (f32[4,384]{1,0:T(4,128)S(1)}, f32[4,384,128]{1,2,0:T(8,128)S(1)}) fusion(bf16[128,128]{1,0:T(8,128)(2,1)} %param.30, f32[4,384,128]{2,1,0:T(8,128)} %reshape.155, f32[4,384,512]{2,1,0:T(8,128)} %copy-done.3, f32[384,128]{0,1:T(8,128)} %copy.37, bf16[4,384,128]{1,2,0:T(8,128)(2,1)} %copy-done.2), kind=kOutput, calls=%fused_computation.165 | convolution fusion | flops 52492800 | bytes 2988032 | tf_op jit(solution)/shard_map/dot_general | solution.py:130
  55.1 0.1 multiply_reduce_fusion
  55.2 0.6 fusion.53
  55.8 0.1 copy-done.8
  56.0 0.0 copy-done.17
  56.0 0.7 fusion.28
  56.6 1.3 %fusion.25 = f32[4,50,768]{2,1,0:T(8,128)S(1)} fusion(bf16[4,384,128]{1,2,0:T(8,128)(2,1)S(1)} %fusion.28, bf16[128,768]{1,0:T(8,128)(2,1)S(1)} %copy-done, s32[384]{0:T(512)S(1)} %broadcast_subtract_fusion, pred[384]{0:T(512)(128)(4,1)S(1)} %copy-done.18), kind=kOutput, calls=%fused_computation.32 | convolution fusion | flops 422352384 | bytes 1206144 | tf_op jit(solution)/shard_map/at,bac->btc/dot_general | solution.py:151
  58.0 1.9 %collective-permute-start.4 = (f32[4,1,768]{2,1,0:T(1,128)S(1)}, f32[4,1,768]{2,1,0:T(1,128)S(1)}, u32[]{:S(2)}, u32[]{:S(2)}) collective-permute-start(f32[4,1,768]{2,1,0:T(1,128)S(1)} %slice.190), channel_id=1, source_target_pairs={{0,1},{1,2},{2,3},{4,5},{5,6},{6,7},{8,9},{9,10},{10,11},{12,13},{... | collective-permute-start | bytes 36872 | tf_op jit(solution)/shard_map/ppermute | solution.py:19
  59.9 0.1 convert_reduce_fusion.3
  60.1 1.0 %collective-permute-done.4 = f32[4,1,768]{2,1,0:T(1,128)S(1)} collective-permute-done((f32[4,1,768]{2,1,0:T(1,128)S(1)}, f32[4,1,768]{2,1,0:T(1,128)S(1)}, u32[]{:S(2)}, u32[]{:S(2)}) %collective-permute-start.4) | collective-permute-done | bytes 12320 | tf_op jit(solution)/shard_map/ppermute | solution.py:19
  61.1 2.1 %collective-permute-start.5 = (f32[4,1,768]{2,1,0:T(1,128)S(1)}, f32[4,1,768]{2,1,0:T(1,128)S(1)}, u32[]{:S(2)}, u32[]{:S(2)}) collective-permute-start(f32[4,1,768]{2,1,0:T(1,128)S(1)} %get-tuple-element.15), channel_id=1, source_target_pairs={{1,0},{2,1},{3,2},{5,4},{6,5},{7,6},{9,8},{10,9},{11,10},{13,12},{... | collective-permute-start | bytes 36872 | tf_op jit(solution)/shard_map/ppermute | solution.py:20
  63.2 0.1 slice_maximum_fusion
  63.3 0.9 %copy.52 = bf16[4,384,128]{2,1,0:T(8,128)(2,1)} copy(bf16[4,384,128]{1,2,0:T(8,128)(2,1)S(1)} %fusion.28) | data formatting | bytes 786432
  64.3 2.1 %collective-permute-done.5 = f32[4,1,768]{2,1,0:T(1,128)S(1)} collective-permute-done((f32[4,1,768]{2,1,0:T(1,128)S(1)}, f32[4,1,768]{2,1,0:T(1,128)S(1)}, u32[]{:S(2)}, u32[]{:S(2)}) %collective-permute-start.5) | collective-permute-done | bytes 12320 | tf_op jit(solution)/shard_map/ppermute | solution.py:20
  66.4 0.8 %fusion.51 = bf16[4,48,768]{2,1,0:T(8,128)(2,1)} fusion(f32[4,1,768]{2,1,0:T(1,128)S(1)} %slice_add_fusion.3, f32[4,46,768]{2,1,0:T(8,128)S(1)} %slice.191, f32[4,1,768]{2,1,0:T(1,128)S(1)} %get-tuple-element.14, f32[48]{0:T(128)S(1)} %slice_maximum_fusion), kind=kLoop, calls=%fused_computation.67 | loop fusion | flops 589824 | bytes 884928 | tf_op jit(solution)/shard_map/convert_element_type | solution.py:166
  (58 shorter events, 0.4 us)
Async XLA Ops:
  0.6 56.0 %copy-start = (bf16[128,768]{1,0:T(8,128)(2,1)S(1)}, bf16[128,768]{1,0:T(8,128)(2,1)}, u32[]{:S(2)}) copy-start(bf16[128,768]{1,0:T(8,128)(2,1)} %param.33) | copy-start | bytes 589828
  0.6 7.2 %copy-start.9 = (bf16[128,512]{1,0:T(8,128)(2,1)S(1)}, bf16[128,512]{1,0:T(8,128)(2,1)}, u32[]{:S(2)}) copy-start(bf16[128,512]{1,0:T(8,128)(2,1)} %param.27) | copy-start | bytes 393220
  6.5 1.4 %copy-start.2 = (bf16[4,384,128]{1,2,0:T(8,128)(2,1)}, bf16[4,384,128]{1,2,0:T(8,128)(2,1)S(1)}, u32[]{:S(2)}) copy-start(bf16[4,384,128]{1,2,0:T(8,128)(2,1)S(1)} %copy.36) | copy-start | bytes 1179652
  7.7 8.2 %copy-start.11 = (s32[384]{0:T(512)S(1)}, s32[384]{0:T(512)}, u32[]{:S(2)}) copy-start(s32[384]{0:T(512)} %param.22) | copy-start | bytes 4612
  7.7 8.2 %copy-start.13 = (s32[384]{0:T(512)S(1)}, s32[384]{0:T(512)}, u32[]{:S(2)}) copy-start(s32[384]{0:T(512)} %param.20) | copy-start | bytes 4612
  7.9 14.4 %copy-start.15 = (f32[128]{0:T(128)S(1)}, f32[128]{0:T(128)}, u32[]{:S(2)}) copy-start(f32[128]{0:T(128)} %param.28) | copy-start | bytes 1540
  8.5 13.8 %copy-start.3 = (f32[4,384,512]{2,1,0:T(8,128)}, f32[4,384,512]{2,1,0:T(8,128)S(1)}, u32[]{:S(2)}) copy-start(f32[4,384,512]{2,1,0:T(8,128)S(1)} %get-tuple-element.31) | copy-start | bytes 9437188
  8.5 15.7 %copy-start.1 = (bf16[12,32,16,128]{3,2,1,0:T(8,128)(2,1)S(1)}, bf16[12,32,16,128]{3,2,1,0:T(8,128)(2,1)}, u32[]{:S(2)}) copy-start(bf16[12,32,16,128]{3,2,1,0:T(8,128)(2,1)} %param.19) | copy-start | bytes 4718596
  9.2 25.4 %collective-permute-start.1 = (bf16[4,48,256]{2,1,0:T(8,128)(2,1)}, bf16[4,48,256]{2,1,0:T(8,128)(2,1)}, u32[]{:S(2)}, u32[]{:S(2)}) collective-permute-start(bf16[4,48,256]{2,1,0:T(8,128)(2,1)} %get-tuple-element.9), channel_id=1, source_target_pairs={{1,0},{2,1},{3,2},{5,4},{6,5},{7,6},{9,8},{10,9},{11,10},{13,12},{... | collective-permute-start | bytes 294920 | tf_op jit(solution)/shard_map/ppermute | solution.py:20
  11.4 23.2 %collective-permute-start = (bf16[4,48,256]{2,1,0:T(8,128)(2,1)}, bf16[4,48,256]{2,1,0:T(8,128)(2,1)}, u32[]{:S(2)}, u32[]{:S(2)}) collective-permute-start(bf16[4,48,256]{2,1,0:T(8,128)(2,1)} %get-tuple-element.8), channel_id=1, source_target_pairs={{0,1},{1,2},{2,3},{4,5},{5,6},{6,7},{8,9},{9,10},{10,11},{12,13},{... | collective-permute-start | bytes 294920 | tf_op jit(solution)/shard_map/ppermute | solution.py:19
  16.7 16.3 %collective-permute-start.3 = (s32[2,48]{1,0:T(2,128)}, s32[2,48]{1,0:T(2,128)S(1)}, u32[]{:S(2)}, u32[]{:S(2)}) collective-permute-start(s32[2,48]{1,0:T(2,128)} %get-tuple-element.21), channel_id=1, source_target_pairs={{1,0},{2,1},{3,2},{5,4},{6,5},{7,6},{9,8},{10,9},{11,10},{13,12},{... | collective-permute-start | bytes 1160 | tf_op jit(solution)/shard_map/ppermute | solution.py:20
  18.6 14.4 %collective-permute-start.2 = (s32[2,48]{1,0:T(2,128)}, s32[2,48]{1,0:T(2,128)}, u32[]{:S(2)}, u32[]{:S(2)}) collective-permute-start(s32[2,48]{1,0:T(2,128)} %get-tuple-element.20), channel_id=1, source_target_pairs={{0,1},{1,2},{2,3},{4,5},{5,6},{6,7},{8,9},{9,10},{10,11},{12,13},{... | collective-permute-start | bytes 1160 | tf_op jit(solution)/shard_map/ppermute | solution.py:19
  22.4 3.6 %copy-start.12 = (f32[4,16]{1,0:T(4,128)S(1)}, f32[4,16]{1,0:T(4,128)}, u32[]{:S(2)}) copy-start(f32[4,16]{1,0:T(4,128)} %param.29) | copy-start | bytes 772
  25.0 4.7 %copy-start.14 = (f32[2,128]{1,0:T(2,128)S(1)}, f32[2,128]{1,0:T(2,128)}, u32[]{:S(2)}) copy-start(f32[2,128]{1,0:T(2,128)} %param.26) | copy-start | bytes 3076
  25.0 4.7 %copy-start.6 = (bf16[384,128]{1,0:T(8,128)(2,1)S(1)}, bf16[384,128]{1,0:T(8,128)(2,1)}, u32[]{:S(2)}) copy-start(bf16[384,128]{1,0:T(8,128)(2,1)} %param.18) | copy-start | bytes 294916
  25.0 4.7 %copy-start.16 = (bf16[2,128,128]{2,1,0:T(8,128)(2,1)S(1)}, bf16[2,128,128]{2,1,0:T(8,128)(2,1)}, u32[]{:S(2)}) copy-start(bf16[2,128,128]{2,1,0:T(8,128)(2,1)} %param.25) | copy-start | bytes 196612
  40.0 2.1 %copy-start.4 = (f32[12,4,32,128]{3,2,1,0:T(8,128)S(1)}, f32[12,4,32,128]{3,2,1,0:T(8,128)}, u32[]{:S(2)}) copy-start(f32[12,4,32,128]{3,2,1,0:T(8,128)} %copy.44) | copy-start | bytes 2359300
  42.0 3.1 %copy-start.5 = (bf16[4,12,128,128]{2,3,1,0:T(8,128)(2,1)S(1)}, bf16[4,12,128,128]{2,3,1,0:T(8,128)(2,1)}, u32[]{:S(2)}) copy-start(bf16[4,12,128,128]{2,3,1,0:T(8,128)(2,1)} %copy.41) | copy-start | bytes 4718596
  53.0 2.2 %copy-start.7 = (f32[384,128]{0,1:T(8,128)S(1)}, f32[384,128]{0,1:T(8,128)}, u32[]{:S(2)}) copy-start(f32[384,128]{0,1:T(8,128)} %copy.48) | copy-start | bytes 589828
  53.0 2.2 %copy-start.10 = (bf16[128,512]{1,0:T(8,128)(2,1)S(1)}, bf16[128,512]{1,0:T(8,128)(2,1)}, u32[]{:S(2)}) copy-start(bf16[128,512]{1,0:T(8,128)(2,1)} %param.31) | copy-start | bytes 393220
  55.0 0.9 %copy-start.8 = (f32[384,128]{0,1:T(8,128)S(1)}, f32[384,128]{0,1:T(8,128)}, u32[]{:S(2)}) copy-start(f32[384,128]{0,1:T(8,128)} %copy.47) | copy-start | bytes 589828
  55.0 0.9 %copy-start.17 = (bf16[256,128]{1,0:T(8,128)(2,1)S(1)}, bf16[256,128]{1,0:T(8,128)(2,1)}, u32[]{:S(2)}) copy-start(bf16[256,128]{1,0:T(8,128)(2,1)} %param.32) | copy-start | bytes 196612
  56.0 0.7 %copy-start.18 = (pred[384]{0:T(512)(128)(4,1)S(1)}, pred[384]{0:T(512)(128)(4,1)}, u32[]{:S(2)}) copy-start(pred[384]{0:T(512)(128)(4,1)} %slice.159) | copy-start | bytes 1156
  58.0 3.1 %collective-permute-start.4 = (f32[4,1,768]{2,1,0:T(1,128)S(1)}, f32[4,1,768]{2,1,0:T(1,128)S(1)}, u32[]{:S(2)}, u32[]{:S(2)}) collective-permute-start(f32[4,1,768]{2,1,0:T(1,128)S(1)} %slice.190), channel_id=1, source_target_pairs={{0,1},{1,2},{2,3},{4,5},{5,6},{6,7},{8,9},{9,10},{10,11},{12,13},{... | collective-permute-start | bytes 36872 | tf_op jit(solution)/shard_map/ppermute | solution.py:19
  61.1 5.2 %collective-permute-start.5 = (f32[4,1,768]{2,1,0:T(1,128)S(1)}, f32[4,1,768]{2,1,0:T(1,128)S(1)}, u32[]{:S(2)}, u32[]{:S(2)}) collective-permute-start(f32[4,1,768]{2,1,0:T(1,128)S(1)} %get-tuple-element.15), channel_id=1, source_target_pairs={{1,0},{2,1},{3,2},{5,4},{6,5},{7,6},{9,8},{10,9},{11,10},{13,12},{... | collective-permute-start | bytes 36872 | tf_op jit(solution)/shard_map/ppermute | solution.py:20
where the time goes:
time: 67.8 us; the launch traced here: 67.2 us
  local copies, waits for them, and re-layouts  19.6 us (29%)
  starting transfers between devices  16.2 us (24%)
  matrix products  14.7 us (22%)
  other arithmetic  11.6 us (17%)
  waiting for transfers between devices  3.13 us (5%)
  between operations  1.9 us (3%)
    ppermute x3, starting transfers between devices, extended_2(): before = lax.ppermute(last, axis, up)  10.1 us
    ppermute x3, starting transfers between devices, extended_2(): after = lax.ppermute(initial, axis, down)  6.16 us
    transpose x1, local copies, waits for them, and re-layouts, on_device(): jnp.einsum('bwhij,bwjhd->bwihd', attention, values_win, preferred_element...  3.28 us
    sub x1, other arithmetic, on_device(): attention = jax.nn.softmax(scores, axis=-1).astype(jnp.bfloat16)  3.04 us
    div x4, local copies, waits for them, and re-layouts, on_device(): jax.nn.sigmoid(jnp.dot(cond_norm, zero_weight[which], preferred_element_t...  2.59 us
    dot_general x1, matrix products, on_device(): jnp.einsum('bwhij,bwjhd->bwihd', attention, values_win, preferred_element...  2.42 us
    unnamed x40, local copies, waits for them, and re-layouts  2.38 us
    dot_general x2, matrix products, on_device(): jnp.dot(cond_norm, ada_weight[which], preferred_element_type=jnp.float32)  2.37 us
  transfers between devices with their start and end apart: 6, of which 2 were waited for; matrix products, arithmetic and copies ran while one was open for 20% of the time, Pallas kernels for 0%

commit v1 on v0

v1 whole, which is shorter than its diff:
```python
import functools

import jax
import jax.numpy as jnp
from jax import lax
from jax.experimental import pallas as pl
from jax.experimental.pallas import tpu as pltpu
from jax.sharding import PartitionSpec as P

ATOMS_PER_TOKEN = 8
EPS = 1e-05
DEAD = -1000000000.0
MESH = pl.DeviceIdType.MESH
F32 = jnp.float32
BF16 = jnp.bfloat16


def iota(shape, axis):
    return lax.broadcasted_iota(jnp.int32, shape, axis)


def mm(a, b):
    return jnp.dot(a, b, preferred_element_type=F32)


def two_pieces(values):
    high = values.astype(BF16)
    low = (values - high.astype(F32)).astype(BF16)
    return high, low


def block_body(
    n,
    atoms_ref, cond_ref, pair_ref, mask_ref, token_ref, count_ref,
    ada_ref, ada_bias_ref, zero_ref, zero_bias_ref, qkvg_ref, query_bias_ref,
    pair_weight_ref, out_ref, swiglu_ref, down_ref, token_weight_ref,
    atoms_out_ref, tokens_out_ref,
    pair_buf, halo_x, halo_c, halo_m, halo_t, kv_ref, q_ref, gate_ref, bias_ref,
    live_ref, mod_ref, feat_ref, center_ref, mean_ref, lhs_ref, fold_ref,
    edge_out, edge_in, onehot_ref, counts_ref,
    pair_sem, send_sem, recv_sem, edge_send_sem, edge_recv_sem,
):
    samples, atoms, width = atoms_ref.shape
    windows, rows_pair, key_len = pair_ref.shape
    heads, channels = pair_weight_ref.shape
    head_dim = width // heads
    query_len = rows_pair // channels
    half = query_len // 2
    margin = (key_len - query_len) // 2
    tokens = tokens_out_ref.shape[1]
    hidden = down_ref.shape[0]
    token_width = token_weight_ref.shape[1]
    rows_half = half * channels

    me = lax.axis_index("atom")
    right, left = lax.rem(me + 1, n), lax.rem(me + n - 1, n)

    groups = pair_sem.shape[0]
    per_group = windows // groups
    pair_copies = []
    for g in range(groups):
        part = pl.ds(g * per_group, per_group)
        copy = pltpu.make_async_copy(pair_ref.at[part], pair_buf.at[part], pair_sem.at[g])
        copy.start()
        pair_copies.append(copy)

    barrier = pltpu.get_barrier_semaphore()
    for neighbour in (left, right):
        pl.semaphore_signal(barrier, inc=1, device_id={"atom": neighbour}, device_id_type=MESH)
    pl.semaphore_wait(barrier, 2)

    copies = []
    for side, (target, start) in enumerate(((right, atoms - margin), (left, 0))):
        own = pl.ds(start, margin)
        for which, (src, dst) in enumerate(
            (
                (atoms_ref.at[:, own], halo_x.at[side]),
                (cond_ref.at[own], halo_c.at[side]),
                (mask_ref, halo_m.at[side]),
                (token_ref, halo_t.at[side]),
            )
        ):
            copy = pltpu.make_async_remote_copy(
                src_ref=src,
                dst_ref=dst,
                send_sem=send_sem.at[side, which],
                recv_sem=recv_sem.at[side, which],
                device_id={"atom": target},
                device_id_type=MESH,
            )
            copy.start()
            copies.append(copy)

    row, col = iota((width, width), 0), iota((width, width), 1)
    inverse = 1.0 / width
    center_ref[...] = (jnp.where(row == col, 1.0, 0.0) - inverse).astype(BF16)
    mean_ref[...] = jnp.full(mean_ref.shape, inverse, F32).astype(BF16)

    def norm(values):
        centred = mm(values, center_ref[...])
        high, low = two_pieces(centred * centred)
        spread = mm(jnp.concatenate([high, low], axis=1), mean_ref[...])
        return centred * lax.rsqrt(spread + EPS)

    cond_norm = norm(cond_ref[...]).astype(BF16)
    for which in range(2):
        adapt = mm(cond_norm, ada_ref[which])
        mod_ref[3 * which] = jax.nn.sigmoid(
            adapt[:, :width] + ada_bias_ref[which : which + 1]
        )
        mod_ref[3 * which + 1] = adapt[:, width:]
        mod_ref[3 * which + 2] = jax.nn.sigmoid(
            mm(cond_norm, zero_ref[which]) + zero_bias_ref[which : which + 1]
        )

    factor = head_dim**-0.5
    kv_ref[:, :, 2 * width :] = jnp.ones((samples, atoms + 2 * margin, width), BF16)
    for s in range(samples):
        attn_in = (norm(atoms_ref[s]) * mod_ref[0] + mod_ref[1]).astype(BF16)
        projected = mm(attn_in, qkvg_ref[...])
        q_ref[s] = ((projected[:, :width] + query_bias_ref[...]) * factor).astype(BF16)
        kv_ref[s, pl.ds(margin, atoms), pl.ds(0, 2 * width)] = projected[
            :, width : 3 * width
        ].astype(BF16)
        gate_ref[s] = jax.nn.sigmoid(projected[:, 3 * width :])

    weight = pair_weight_ref[...]
    weight = weight - jnp.mean(weight, axis=1, keepdims=True)
    row, col = iota((rows_half, rows_half), 0), iota((rows_half, rows_half), 1)
    same = jnp.where(row // channels == col // channels, 1.0 / channels, 0.0)
    lhs_ref[pl.ds(0, rows_half)] = (jnp.where(row == col, 1.0, 0.0) - same).astype(BF16)
    spread_c = jnp.where(
        iota((channels, rows_half), 1) % channels == iota((channels, rows_half), 0), 1.0, 0.0
    ).astype(BF16)
    own_query = iota((half, rows_half), 1) // channels == iota((half, rows_half), 0)
    remaining = weight
    lines = heads * half
    for piece in range(3):
        part = remaining.astype(BF16)
        remaining = remaining - part.astype(F32)
        wide = mm(part, spread_c)
        blocks = [
            jnp.where(own_query, jnp.broadcast_to(wide[h : h + 1], (half, rows_half)), 0.0)
            for h in range(heads)
        ]
        lhs_ref[pl.ds(rows_half + piece * lines, lines)] = jnp.concatenate(
            blocks, axis=0
        ).astype(BF16)
    folded = rows_half // 2
    fold_ref[...] = jnp.where(
        (iota((half, 2 * folded), 1) % folded) // (channels // 2) == iota((half, 2 * folded), 0),
        1.0 / channels,
        0.0,
    ).astype(BF16)

    def pair_window(w):
        block = pair_buf[w]
        both = jnp.concatenate([block[:rows_half], block[rows_half:]], axis=1)
        result = mm(lhs_ref[...], both)
        centred = result[:rows_half]
        at = rows_half
        total = (
            result[at : at + lines]
            + result[at + lines : at + 2 * lines]
            + result[at + 2 * lines : at + 3 * lines]
        )
        square = (centred * centred).reshape(half, 2, channels // 2, 2 * key_len)
        square = (square[:, 0] + square[:, 1]).reshape(folded, 2 * key_len)
        high, low = two_pieces(square)
        spread = mm(fold_ref[...], jnp.concatenate([high, low], axis=0))
        scale = lax.rsqrt(spread + EPS)
        bias = total * jnp.concatenate([scale] * heads, axis=0)
        bias_ref[w, pl.ds(0, lines)] = bias[:, :key_len]
        bias_ref[w, pl.ds(lines, lines)] = bias[:, key_len:]

    for g in range(groups):
        pair_copies[g].wait()

        def pair_step(i, carry, g=g):
            pair_window(g * per_group + 2 * i)
            pair_window(g * per_group + 2 * i + 1)
            return carry

        lax.fori_loop(0, per_group // 2, pair_step, 0)

    for copy in copies:
        copy.wait()
    lanes = 128
    mask_ext = jnp.concatenate(
        [halo_m[0][:, atoms - lanes :], mask_ref[...], halo_m[1][:, :lanes]], axis=1
    )
    token_ext = jnp.concatenate(
        [halo_t[0][:, atoms - lanes :], token_ref[...], halo_t[1][:, :lanes]], axis=1
    )
    extent = atoms + 2 * lanes
    position = me * atoms - lanes + iota((1, extent), 1)
    usable = (
        (mask_ext == 1)
        & (position >= 0)
        & (position < n * atoms)
        & (position < count_ref[0])
    )
    live = jnp.broadcast_to(jnp.where(usable, 1.0, 0.0), (8, extent))
    for w in range(windows):
        shift = (extent - (lanes - margin + query_len * w)) % extent
        live_ref[w] = pltpu.roll(live, shift, axis=1)[:, :key_len]
    relative = jnp.where(usable, token_ext - me * tokens, -2)
    hits = iota((tokens, extent), 0) == jnp.broadcast_to(relative, (tokens, extent))
    hits = jnp.where(hits, 1.0, 0.0)
    counts_ref[...] = jnp.broadcast_to(
        1.0 / jnp.maximum(jnp.sum(hits, axis=1, keepdims=True), 1.0), counts_ref.shape
    )
    onehot_ref[...] = hits[:, lanes : lanes + atoms].astype(BF16)
    relative8 = jnp.broadcast_to(relative[:, lanes : lanes + atoms], (8, atoms))
    rolled8 = pltpu.roll(relative8, query_len, axis=1)
    lower_hit = jnp.where(relative8[:, :lanes] == -1, 1.0, 0.0).astype(BF16)[:, :query_len]
    upper_hit = jnp.where(rolled8[:, :lanes] == tokens, 1.0, 0.0).astype(BF16)[:, :query_len]

    for side in range(2):
        inside = (me > 0) if side == 0 else (me < n - 1)
        cond_halo = norm(halo_c[side]).astype(BF16)
        adapt = mm(cond_halo, ada_ref[0])
        scale = jax.nn.sigmoid(adapt[:, :width] + ada_bias_ref[0:1])
        shift = adapt[:, width:]
        normed = norm(halo_x[side].reshape(samples * margin, width))
        attn_in = (normed.reshape(samples, margin, width) * scale[None] + shift[None]).astype(BF16)
        projected = mm(
            attn_in.reshape(samples * margin, width), qkvg_ref[:, pl.ds(width, 2 * width)]
        )
        projected = jnp.where(inside, projected, 0.0).astype(BF16)
        start = 0 if side == 0 else margin + atoms
        kv_ref[:, pl.ds(start, margin), pl.ds(0, 2 * width)] = projected.reshape(
            samples, margin, 2 * width
        )

    head_of = iota((half, width), 1) // head_dim

    def attend(s, w):
        rows = pl.ds(pl.multiple_of(w * query_len, query_len), query_len)
        keys = pl.ds(pl.multiple_of(w * query_len, query_len), key_len)
        query = q_ref[s, rows]
        parts = []
        for side in range(2):
            piece = query[side * half : (side + 1) * half]
            for h in range(heads):
                parts.append(jnp.where(head_of == h, piece, jnp.zeros_like(piece)))
        stacked = jnp.concatenate(parts, axis=0)
        scores = lax.dot_general(
            stacked,
            kv_ref[s, keys, pl.ds(0, width)],
            (((1,), (1,)), ((), ())),
            preferred_element_type=F32,
        )
        scores = jnp.where(live_ref[w][0:1] > 0.5, scores + bias_ref[w], DEAD)
        top = jnp.max(scores, axis=1, keepdims=True)
        weights = jnp.exp(scores - top).astype(BF16)
        mixed = mm(weights, kv_ref[s, keys, pl.ds(width, 2 * width)])
        outs = []
        for side in range(2):
            base = side * heads * half
            value = mixed[base : base + half, :width]
            amount = mixed[base : base + half, width:]
            for h in range(1, heads):
                at = base + h * half
                value = jnp.where(head_of == h, mixed[at : at + half, :width], value)
                amount = jnp.where(head_of == h, mixed[at : at + half, width:], amount)
            outs.append(value / amount)
        return (jnp.concatenate(outs, axis=0) * gate_ref[s, rows]).astype(BF16)

    def process(pairs):
        rows = [pl.ds(pl.multiple_of(w * query_len, query_len), query_len) for w in pairs]
        order = [(s, i) for s in range(samples) for i in range(len(pairs))]

        def modulation(k):
            one = jnp.concatenate([mod_ref[k, r] for r in rows], axis=0)
            return jnp.concatenate([one] * samples, axis=0)

        blended = jnp.concatenate([attend(s, pairs[i]) for s, i in order], axis=0)
        stream = jnp.concatenate([atoms_ref[s, rows[i]] for s, i in order], axis=0).astype(F32)
        after = (stream + modulation(2) * mm(blended, out_ref[...])).astype(BF16)
        trans_in = (norm(after) * modulation(3) + modulation(4)).astype(BF16)
        mixed = mm(trans_in, swiglu_ref[...])
        units = (jax.nn.silu(mixed[:, :hidden]) * mixed[:, hidden:]).astype(BF16)
        final = (after.astype(F32) + modulation(5) * mm(units, down_ref[...])).astype(BF16)
        features = jnp.maximum(mm(final, token_weight_ref[...]), 0.0).astype(BF16)
        for place, (s, i) in enumerate(order):
            at = place * query_len
            atoms_out_ref[s, rows[i]] = final[at : at + query_len]
            feat_ref[s, rows[i]] = features[at : at + query_len]
        return features

    features = process([0, windows - 1])
    sample_row = iota((8, token_width), 0)
    for side, hit in enumerate((upper_hit, lower_hit)):
        place = 1 - side
        total = jnp.zeros((8, token_width), F32)
        for s in range(samples):
            at = (2 * s + place) * query_len
            total = jnp.where(sample_row == s, mm(hit, features[at : at + query_len]), total)
        edge_out[side] = total
    edge_copies = []
    for side, target in enumerate((right, left)):
        copy = pltpu.make_async_remote_copy(
            src_ref=edge_out.at[side],
            dst_ref=edge_in.at[side],
            send_sem=edge_send_sem.at[side],
            recv_sem=edge_recv_sem.at[side],
            device_id={"atom": target},
            device_id_type=MESH,
        )
        copy.start()
        edge_copies.append(copy)

    def middle(i, carry):
        process([2 * i + 1, 2 * i + 2])
        return carry

    lax.fori_loop(0, (windows - 2) // 2, middle, 0)

    for copy in edge_copies:
        copy.wait()
    token_row = iota((tokens, token_width), 0)
    per_count = counts_ref[:, 0:1]
    for s in range(samples):
        total = mm(onehot_ref[...], feat_ref[s])
        from_left = jnp.where(me > 0, edge_in[0, s : s + 1], 0.0)
        from_right = jnp.where(me < n - 1, edge_in[1, s : s + 1], 0.0)
        total = total + jnp.where(token_row == 0, from_left, 0.0)
        total = total + jnp.where(token_row == tokens - 1, from_right, 0.0)
        tokens_out_ref[s] = (total * per_count).astype(BF16)


def on_device(
    n,
    atoms_in, cond, pair, atom_mask, atom_count, atom_to_token, ada_weight, ada_bias,
    zero_weight, zero_bias, qkvg_weight, query_bias, pair_weight, out_weight,
    swiglu_weight, down_weight, token_weight,
):
    samples, atoms, width = atoms_in.shape
    windows, query_len, channels, key_len = pair.shape
    heads = pair_weight.shape[0]
    margin = (key_len - query_len) // 2
    tokens = atoms // ATOMS_PER_TOKEN
    token_width = token_weight.shape[1]
    half = query_len // 2
    rows_half = half * channels
    groups = 3 if windows % 6 == 0 else 1
    vmem = pl.BlockSpec(memory_space=pltpu.VMEM)
    smem = pl.BlockSpec(memory_space=pltpu.SMEM)
    return pl.pallas_call(
        functools.partial(block_body, n),
        out_shape=(
            jax.ShapeDtypeStruct(atoms_in.shape, BF16),
            jax.ShapeDtypeStruct((samples, tokens, token_width), BF16),
        ),
        in_specs=[vmem, vmem, pl.BlockSpec(memory_space=pl.ANY), vmem, vmem, smem] + [vmem] * 11,
        out_specs=(vmem, vmem),
        scratch_shapes=[
            pltpu.VMEM((windows, query_len * channels, key_len), BF16),
            pltpu.VMEM((2, samples, margin, width), BF16),
            pltpu.VMEM((2, margin, width), BF16),
            pltpu.VMEM((2, 1, atoms), jnp.int32),
            pltpu.VMEM((2, 1, atoms), jnp.int32),
            pltpu.VMEM((samples, atoms + 2 * margin, 3 * width), BF16),
            pltpu.VMEM((samples, atoms, width), BF16),
            pltpu.VMEM((samples, atoms, width), F32),
            pltpu.VMEM((windows, heads * query_len, key_len), F32),
            pltpu.VMEM((windows, 8, key_len), F32),
            pltpu.VMEM((6, atoms, width), F32),
            pltpu.VMEM((samples, atoms, token_width), BF16),
            pltpu.VMEM((width, width), BF16),
            pltpu.VMEM((2 * width, width), BF16),
            pltpu.VMEM((rows_half + 3 * heads * half, rows_half), BF16),
            pltpu.VMEM((half, rows_half), BF16),
            pltpu.VMEM((2, 8, token_width), F32),
            pltpu.VMEM((2, 8, token_width), F32),
            pltpu.VMEM((tokens, atoms), BF16),
            pltpu.VMEM((tokens, 128), F32),
            pltpu.SemaphoreType.DMA((groups,)),
            pltpu.SemaphoreType.DMA((2, 4)),
            pltpu.SemaphoreType.DMA((2, 4)),
            pltpu.SemaphoreType.DMA((2,)),
            pltpu.SemaphoreType.DMA((2,)),
        ],
        compiler_params=pltpu.CompilerParams(collective_id=0, has_side_effects=True),
        name="atom_block",
    )(
        atoms_in, cond, pair.reshape(windows, query_len * channels, key_len),
        atom_mask.reshape(1, atoms), atom_to_token.reshape(1, atoms), atom_count,
        ada_weight, ada_bias, zero_weight, zero_bias, qkvg_weight,
        query_bias.reshape(1, width), pair_weight, out_weight, swiglu_weight,
        down_weight, token_weight,
    )


def solution(mesh):
    shard = P(("struct", "atom"))
    stream = P("struct", "atom", None)
    in_specs = (stream, shard, shard, shard, P("struct"), shard) + (P(),) * 11
    return jax.shard_map(
        functools.partial(on_device, mesh.shape["atom"]),
        mesh=mesh,
        in_specs=in_specs,
        out_specs=(stream, stream),
        check_vma=False,
    )
```

time: 67.8 us -> 36.2 us (0.53)
  Pallas kernels: 0 us -> 28.7 us
  starting transfers between devices: 16.2 us -> 0 us
  matrix products: 14.7 us -> 0 us
  local copies, waits for them, and re-layouts: 19.6 us -> 5.95 us
  other arithmetic: 11.6 us -> 0 us
  waiting for transfers between devices: 3.13 us -> 0 us
    pallas_call x0 -> x1, Pallas kernels: none -> 28.7 us  [on_device(): pl.pallas_call(functools.partial(block_body, n), out_shape=(jax.ShapeDtyp...]
    ppermute x6 -> x0, starting transfers between devices: 16.2 us -> none  [the longest x3 10.1 us: extended_2(): before = lax.ppermute(last, axis, up)]
    dot_general x12 -> x0, matrix products: 14.7 us -> none  [the longest x1 2.42 us: on_device(): jnp.einsum('bwhij,bwjhd->bwihd', attention, values_win, preferred_element...]
    slice x12 -> x0, local copies, waits for them, and re-layouts: 5.53 us -> none  [the longest x2 1.8 us: on_device(): windowed[..., :model_width]]
    reduce_sum x8 -> x0, other arithmetic: 4.3 us -> none  [the longest x4 2.3 us: layer_norm(): spread = jnp.mean(jnp.square(values - center), along, keepdims=True)]
    transpose x2 -> x0, local copies, waits for them, and re-layouts: 4.26 us -> none  [the longest x1 3.28 us: on_device(): jnp.einsum('bwhij,bwjhd->bwihd', attention, values_win, preferred_element...]
    ppermute x6 -> x0, waiting for transfers between devices: 3.13 us -> none  [the longest x3 2.11 us: extended_2(): after = lax.ppermute(initial, axis, down)]
    sub x3 -> x0, other arithmetic: 3.05 us -> none  [the longest x1 3.04 us: on_device(): attention = jax.nn.softmax(scores, axis=-1).astype(jnp.bfloat16)]
  transfers between devices with their start and end apart: 6 -> 0, of which waited for: 2 -> 0; matrix products, arithmetic and copies ran while one was open for 20% -> 0% of each run, Pallas kernels for 0% -> 0%
where the time goes in v1:
time: 36.2 us; the launch traced here: 35.9 us
  Pallas kernels  28.7 us (79%)
  local copies, waits for them, and re-layouts  5.95 us (16%)
  between operations  1.29 us (4%)
    pallas_call x1, Pallas kernels, on_device(): pl.pallas_call(functools.partial(block_body, n), out_shape=(jax.ShapeDtyp...  28.7 us
    unnamed x2, local copies, waits for them, and re-layouts  3.46 us
    reshape x1, local copies, waits for them, and re-layouts, on_device(): atom_mask.reshape(1, atoms)  1.25 us
    reshape x1, local copies, waits for them, and re-layouts, on_device(): atom_to_token.reshape(1, atoms)  1.24 us

profile of v1, /device:TPU:1, one launch (start us, length us, event | category | flops | bytes accessed | tf_op | source)
XLA Modules:
  0.0 35.9 jit_solution(4001398434721526568)
XLA Ops:
  1.3 1.2 %reshape.17.mask_ref = s32[1,384]{1,0:T(1,128)} reshape(s32[384]{0:T(512)} %param.20) | data formatting | bytes 3072 | tf_op jit(solution)/shard_map/reshape | solution.py:389
  2.5 1.2 %reshape.18.token_ref = s32[1,384]{1,0:T(1,128)} reshape(s32[384]{0:T(512)} %param.22) | data formatting | bytes 3072 | tf_op jit(solution)/shard_map/reshape | solution.py:389
  3.8 28.7 %atom_block.1 = (bf16[4,384,128]{2,1,0:T(8,128)(2,1)}, bf16[4,48,768]{2,1,0:T(8,128)(2,1)}) custom-call(bf16[4,384,128]{2,1,0:T(8,128)(2,1)} %atoms_ref.1, bf16[384,128]{1,0:T(8,128)(2,1)} %cond_ref.1, bf16[12,512,128]{2,1,0:T(8,128)(2,1)} %bitcast.2, s32[1,384]{1,0:T(1,128)} %reshape.17.mask_ref, s32[1,384]{1,0:T(1,128)} %reshape.18.token_ref, ...), custom_call_target="tpu_custom_call" | custom-call | tf_op jit(solution)/shard_map/atom_block/pallas_call | solution.py:350
  32.5 1.8 %copy.22 = bf16[4,384,128]{2,1,0:T(8,128)(2,1)} copy(bf16[4,384,128]{2,1,0:T(8,128)(2,1)} %get-tuple-element.4) | data formatting | bytes 786432
  34.2 1.7 %copy.23 = bf16[4,48,768]{2,1,0:T(8,128)(2,1)} copy(bf16[4,48,768]{2,1,0:T(8,128)(2,1)} %get-tuple-element.5) | data formatting | bytes 589824

commit v2 on v1

--- a/solution.py
+++ b/solution.py
@@ -9,6 +9,7 @@
 
 ATOMS_PER_TOKEN = 8
 EPS = 1e-05
+STEPS = 1
 DEAD = -1000000000.0
 MESH = pl.DeviceIdType.MESH
 F32 = jnp.float32
@@ -31,14 +32,16 @@
 
 def block_body(
     n,
-    atoms_ref, cond_ref, pair_ref, mask_ref, token_ref, count_ref,
-    ada_ref, ada_bias_ref, zero_ref, zero_bias_ref, qkvg_ref, query_bias_ref,
-    pair_weight_ref, out_ref, swiglu_ref, down_ref, token_weight_ref,
+    atoms_hbm, cond_hbm, pair_ref, mask_ref, token_ref, count_ref,
+    ada_hbm, ada_bias_hbm, zero_hbm, zero_bias_hbm, qkvg_hbm, query_bias_hbm,
+    pair_weight_hbm, out_hbm, swiglu_hbm, down_hbm, token_weight_hbm,
     atoms_out_ref, tokens_out_ref,
-    pair_buf, halo_x, halo_c, halo_m, halo_t, kv_ref, q_ref, gate_ref, bias_ref,
+    atoms_ref, cond_ref, ada_ref, ada_bias_ref, zero_ref, zero_bias_ref, qkvg_ref,
+    query_bias_ref, pair_weight_ref, out_ref, swiglu_ref, down_ref, token_weight_ref,
+    pair_buf, halo_x, halo_c, halo_m0, halo_m1, halo_t0, halo_t1, kv_ref, q_ref, gate_ref, bias_ref,
     live_ref, mod_ref, feat_ref, center_ref, mean_ref, lhs_ref, fold_ref,
     edge_out, edge_in, onehot_ref, counts_ref,
-    pair_sem, send_sem, recv_sem, edge_send_sem, edge_recv_sem,
+    load_sem, pair_sem, send_sem, recv_sem, edge_send_sem, edge_recv_sem,
 ):
     samples, atoms, width = atoms_ref.shape
     windows, rows_pair, key_len = pair_ref.shape
@@ -52,9 +55,26 @@
     token_width = token_weight_ref.shape[1]
     rows_half = half * channels
 
+    halo_m, halo_t = (halo_m0, halo_m1), (halo_t0, halo_t1)
     me = lax.axis_index("atom")
     right, left = lax.rem(me + 1, n), lax.rem(me + n - 1, n)
 
+    early = (
+        (cond_hbm, cond_ref), (atoms_hbm, atoms_ref), (ada_hbm, ada_ref),
+        (ada_bias_hbm, ada_bias_ref), (zero_hbm, zero_ref), (zero_bias_hbm, zero_bias_ref),
+        (qkvg_hbm, qkvg_ref), (query_bias_hbm, query_bias_ref),
+        (pair_weight_hbm, pair_weight_ref),
+    )
+    late = (
+        (out_hbm, out_ref), (swiglu_hbm, swiglu_ref), (down_hbm, down_ref),
+        (token_weight_hbm, token_weight_ref),
+    )
+    loads = [
+        pltpu.make_async_copy(src, dst, load_sem.at[i])
+        for i, (src, dst) in enumerate(early + late)
+    ]
+    for copy in loads[: len(early)]:
+        copy.start()
     groups = pair_sem.shape[0]
     per_group = windows // groups
     pair_copies = []
@@ -63,6 +83,8 @@
         copy = pltpu.make_async_copy(pair_ref.at[part], pair_buf.at[part], pair_sem.at[g])
         copy.start()
         pair_copies.append(copy)
+    for copy in loads[len(early) :]:
+        copy.start()
 
     barrier = pltpu.get_barrier_semaphore()
     for neighbour in (left, right):
@@ -74,10 +96,10 @@
         own = pl.ds(start, margin)
         for which, (src, dst) in enumerate(
             (
-                (atoms_ref.at[:, own], halo_x.at[side]),
-                (cond_ref.at[own], halo_c.at[side]),
-                (mask_ref, halo_m.at[side]),
-                (token_ref, halo_t.at[side]),
+                (atoms_hbm.at[:, own], halo_x.at[side]),
+                (cond_hbm.at[own], halo_c.at[side]),
+                (mask_ref, halo_m[side]),
+                (token_ref, halo_t[side]),
             )
         ):
             copy = pltpu.make_async_remote_copy(
@@ -95,6 +117,9 @@
     inverse = 1.0 / width
     center_ref[...] = (jnp.where(row == col, 1.0, 0.0) - inverse).astype(BF16)
     mean_ref[...] = jnp.full(mean_ref.shape, inverse, F32).astype(BF16)
+
+    for copy in loads[: len(early)]:
+        copy.wait()
 
     def norm(values):
         centred = mm(values, center_ref[...])
@@ -186,11 +211,17 @@
     for copy in copies:
         copy.wait()
     lanes = 128
+
+    def as_row(ref):
+        return ref[...].reshape(1, atoms)
+
     mask_ext = jnp.concatenate(
-        [halo_m[0][:, atoms - lanes :], mask_ref[...], halo_m[1][:, :lanes]], axis=1
+        [as_row(halo_m[0])[:, atoms - lanes :], as_row(mask_ref), as_row(halo_m[1])[:, :lanes]],
+        axis=1,
     )
     token_ext = jnp.concatenate(
-        [halo_t[0][:, atoms - lanes :], token_ref[...], halo_t[1][:, :lanes]], axis=1
+        [as_row(halo_t[0])[:, atoms - lanes :], as_row(token_ref), as_row(halo_t[1])[:, :lanes]],
+        axis=1,
     )
     extent = atoms + 2 * lanes
     position = me * atoms - lanes + iota((1, extent), 1)
@@ -288,6 +319,9 @@
             atoms_out_ref[s, rows[i]] = final[at : at + query_len]
             feat_ref[s, rows[i]] = features[at : at + query_len]
         return features
+
+    for copy in loads[len(early) :]:
+        copy.wait()
 
     features = process([0, windows - 1])
     sample_row = iota((8, token_width), 0)
@@ -312,10 +346,11 @@
         edge_copies.append(copy)
 
     def middle(i, carry):
-        process([2 * i + 1, 2 * i + 2])
+        process([per_step * i + 1 + j for j in range(per_step)])
         return carry
 
-    lax.fori_loop(0, (windows - 2) // 2, middle, 0)
+    per_step = (windows - 2) // STEPS
+    lax.fori_loop(0, STEPS, middle, 0)
 
     for copy in edge_copies:
         copy.wait()
@@ -346,21 +381,30 @@
     rows_half = half * channels
     groups = 3 if windows % 6 == 0 else 1
     vmem = pl.BlockSpec(memory_space=pltpu.VMEM)
+    hbm = pl.BlockSpec(memory_space=pltpu.HBM)
+    query_bias = query_bias.reshape(1, width)
+    staged = (
+        atoms_in, cond, ada_weight, ada_bias, zero_weight, zero_bias, qkvg_weight,
+        query_bias, pair_weight, out_weight, swiglu_weight, down_weight, token_weight,
+    )
     smem = pl.BlockSpec(memory_space=pltpu.SMEM)
     return pl.pallas_call(
         functools.partial(block_body, n),
         out_shape=(
-            jax.ShapeDtypeStruct(atoms_in.shape, BF16),
-            jax.ShapeDtypeStruct((samples, tokens, token_width), BF16),
+            pltpu.VMEM(atoms_in.shape, BF16),
+            pltpu.VMEM((samples, tokens, token_width), BF16),
         ),
-        in_specs=[vmem, vmem, pl.BlockSpec(memory_space=pl.ANY), vmem, vmem, smem] + [vmem] * 11,
+        in_specs=[hbm, hbm, hbm, vmem, vmem, smem] + [hbm] * 11,
         out_specs=(vmem, vmem),
-        scratch_shapes=[
+        scratch_shapes=[pltpu.VMEM(a.shape, a.dtype) for a in staged]
+        + [
             pltpu.VMEM((windows, query_len * channels, key_len), BF16),
             pltpu.VMEM((2, samples, margin, width), BF16),
             pltpu.VMEM((2, margin, width), BF16),
-            pltpu.VMEM((2, 1, atoms), jnp.int32),
-            pltpu.VMEM((2, 1, atoms), jnp.int32),
+            pltpu.VMEM((atoms,), jnp.int32),
+            pltpu.VMEM((atoms,), jnp.int32),
+            pltpu.VMEM((atoms,), jnp.int32),
+            pltpu.VMEM((atoms,), jnp.int32),
             pltpu.VMEM((samples, atoms + 2 * margin, 3 * width), BF16),
             pltpu.VMEM((samples, atoms, width), BF16),
             pltpu.VMEM((samples, atoms, width), F32),
@@ -376,6 +420,7 @@
             pltpu.VMEM((2, 8, token_width), F32),
             pltpu.VMEM((tokens, atoms), BF16),
             pltpu.VMEM((tokens, 128), F32),
+            pltpu.SemaphoreType.DMA((len(staged),)),
             pltpu.SemaphoreType.DMA((groups,)),
             pltpu.SemaphoreType.DMA((2, 4)),
             pltpu.SemaphoreType.DMA((2, 4)),
@@ -386,9 +431,9 @@
         name="atom_block",
     )(
         atoms_in, cond, pair.reshape(windows, query_len * channels, key_len),
-        atom_mask.reshape(1, atoms), atom_to_token.reshape(1, atoms), atom_count,
+        atom_mask, atom_to_token, atom_count,
         ada_weight, ada_bias, zero_weight, zero_bias, qkvg_weight,
-        query_bias.reshape(1, width), pair_weight, out_weight, swiglu_weight,
+        query_bias, pair_weight, out_weight, swiglu_weight,
         down_weight, token_weight,
     )
 

time: 36.2 us -> 27.1 us (0.75)
  Pallas kernels: 28.7 us -> 24.2 us
  local copies, waits for them, and re-layouts: 5.95 us -> 1.46 us
    pallas_call x1, Pallas kernels: 28.7 us -> 24.2 us  [on_device(): pl.pallas_call(functools.partial(block_body, n), out_shape=(pltpu.VMEM(at...]
    reshape x2 -> x0, local copies, waits for them, and re-layouts: 2.49 us -> none  [the longest x1 1.25 us: on_device(): atom_mask.reshape(1, atoms)]
    unnamed x2, local copies, waits for them, and re-layouts: 3.46 us -> 1.46 us
where the time goes in v2:
time: 27.1 us; the launch traced here: 27 us
  Pallas kernels  24.2 us (89%)
  local copies, waits for them, and re-layouts  1.46 us (5%)
  between operations  1.29 us (5%)
    pallas_call x1, Pallas kernels, on_device(): pl.pallas_call(functools.partial(block_body, n), out_shape=(pltpu.VMEM(at...  24.2 us
    unnamed x2, local copies, waits for them, and re-layouts  1.46 us

profile of v2, /device:TPU:1, one launch (start us, length us, event | category | flops | bytes accessed | tf_op | source)
XLA Modules:
  0.0 27.0 jit_solution(4153631497515020968)
XLA Ops:
  1.3 24.2 %atom_block.1 = (bf16[4,384,128]{2,1,0:T(8,128)(2,1)S(1)}, bf16[4,48,768]{2,1,0:T(8,128)(2,1)S(1)}) custom-call(bf16[4,384,128]{2,1,0:T(8,128)(2,1)} %atoms_hbm.1, bf16[384,128]{1,0:T(8,128)(2,1)} %cond_hbm.1, bf16[12,512,128]{2,1,0:T(8,128)(2,1)} %bitcast.2, s32[384]{0:T(512)} %mask_ref.1, s32[384]{0:T(512)} %token_ref.1, s32[1]{0:T(128)S(6)} %copy.23.count_ref, ...), custom_call_target="tpu_custom_call" | custom-call | tf_op jit(solution)/shard_map/atom_block/pallas_call | solution.py:391
  25.5 0.7 %copy.21 = bf16[4,384,128]{2,1,0:T(8,128)(2,1)} copy(bf16[4,384,128]{2,1,0:T(8,128)(2,1)S(1)} %get-tuple-element.2) | data formatting | bytes 786432
  26.2 0.7 %copy.22 = bf16[4,48,768]{2,1,0:T(8,128)(2,1)} copy(bf16[4,48,768]{2,1,0:T(8,128)(2,1)S(1)} %get-tuple-element.3) | data formatting | bytes 589824
